TPU v7x, 32 devices: a whole 2x2x4 slice. The times are simulated.
32 devices in a mesh: section: 4 (over x, core), dp: 8 (over z, y).
Axes of the slice: x: 2, y: 2, z: 4, core: 2. Of those that a mesh axis runs over, the one named last changes fastest.
Arguments:
- obs_features: bfloat16 [4, 256, 1024], P(None, 'dp'), may hold values from -1.1953125 to 1.1953125
- w_input: bfloat16 [4, 1024, 4096], P('section'), may hold values from -1 to 1
- w_recurrent: bfloat16 [4, 1024, 4096], P('section', None, 'dp'), may hold values from -0.1875 to 0.1875
- bias: float32 [4, 4096], P('section'), may hold values from -3 to 3
- stored_states: bfloat16 [4, 4, 256, 2048], P('section', None, 'dp'), may hold values from -3 to 3
- state_owner: int32 [256], P('dp'), may hold values from 0 to 3
- burn_steps: int32 [256], P('dp'), may hold values from 1 to 2
- valid_steps: int32 [256], P('dp'), may hold values from 3 to 4
- cotangent: bfloat16 [4, 256, 1024], P(None, 'dp'), may hold values from -3 to 3
Outputs:
- hidden_all: bfloat16 [4, 4, 256, 1024], P('section', None, 'dp')
- grad_recurrent: float32 [4, 1024, 4096], P('section', None, 'dp')
- grad_bias: float32 [4, 4096], P('section', 'dp')
All inputs are finite; a program needn't handle non-finite values.
Results may differ from a plain program's by a relative error of at most 0.017.
Values may be sent and summed in bfloat16 or wider, within the bound.
No kernel may reach another device: no remote copies, remote signals or barrier semaphores. Data moves between devices by JAX's collectives and lax.ppermute only.
A program may use at most 128 MiB of HBM per device.

v0:
```python
from functools import partial
import jax
import jax.numpy as jnp
from jax import lax
from jax.sharding import PartitionSpec as P


def from_behind(array, axis, by):
    peers = lax.axis_size(axis)
    pairs = [(i, i + by) for i in range(peers) if 0 <= i + by < peers]
    return lax.ppermute(array, axis, pairs)


def lstm_cell(preact, cell_prev):
    breadth = cell_prev.shape[-1]
    in_gate = jax.nn.sigmoid(preact[:, :breadth])
    forget = jax.nn.sigmoid(preact[:, breadth : 2 * breadth])
    candidate = jnp.tanh(preact[:, 2 * breadth : 3 * breadth])
    out_gate = jax.nn.sigmoid(preact[:, 3 * breadth :])
    cell_new = forget * cell_prev + in_gate * candidate
    hidden_new = (out_gate * jnp.tanh(cell_new)).astype(jnp.bfloat16)
    gate_vals = jnp.concatenate([in_gate, forget, candidate, out_gate], axis=-1)
    return (hidden_new, cell_new, gate_vals)


def forward_span(inputs, w_in, w_rec, bias_row, hidden_start, cell_start):
    step_count, seq_rows, breadth = inputs.shape
    projected = jnp.dot(
        inputs.reshape(step_count * seq_rows, breadth), w_in, preferred_element_type=jnp.float32
    )
    projected = projected.reshape(step_count, seq_rows, -1) + bias_row

    def advance(carried, proj_row):
        hidden_prev, cell_prev = carried
        preact = proj_row + jnp.dot(hidden_prev, w_rec, preferred_element_type=jnp.float32)
        hidden_new, cell_new, gate_vals = lstm_cell(preact, cell_prev)
        return ((hidden_new, cell_new), (hidden_new, cell_new, gate_vals))

    (hidden_end, cell_end), (hidden_seq, cell_seq, gate_seq) = lax.scan(
        advance, (hidden_start, cell_start), projected
    )
    return (hidden_seq, cell_seq, gate_seq, hidden_end, cell_end)


def times_transposed(operand, matrix):
    return lax.dot_general(
        operand, matrix, (((1,), (1,)), ((), ())), preferred_element_type=jnp.float32
    )


def backward_span(above_grads, cell_now, cell_old, gate_seq, live_mask, w_rec, grad_h, grad_c):

    def retreat(carried, inputs):
        grad_hidden, grad_cell = carried
        grad_out, cell_cur, cell_before, gate_vals, alive_row = inputs
        breadth = cell_cur.shape[-1]
        in_gate = gate_vals[:, :breadth]
        forget = gate_vals[:, breadth : 2 * breadth]
        candidate = gate_vals[:, 2 * breadth : 3 * breadth]
        out_gate = gate_vals[:, 3 * breadth :]
        total_h = grad_out.astype(jnp.float32) + grad_hidden
        squashed = jnp.tanh(cell_cur)
        total_c = grad_cell + total_h * out_gate * (1.0 - squashed * squashed)
        grad_pre = (
            jnp.concatenate(
                [
                    total_c * candidate * in_gate * (1.0 - in_gate),
                    total_c * cell_before * forget * (1.0 - forget),
                    total_c * in_gate * (1.0 - candidate * candidate),
                    total_h * squashed * out_gate * (1.0 - out_gate),
                ],
                axis=-1,
            )
            * alive_row[:, None]
        )
        gate_grads = grad_pre.astype(jnp.bfloat16)
        return (
            (times_transposed(gate_grads, w_rec), total_c * forget * alive_row[:, None]),
            gate_grads,
        )

    (grad_h_end, grad_c_end), gate_grads = lax.scan(
        retreat,
        (grad_h, grad_c),
        (above_grads, cell_now, cell_old, gate_seq, live_mask),
        reverse=True,
    )
    return (gate_grads, grad_h_end, grad_c_end)


def on_device(
    obs_features,
    w_input,
    w_recurrent,
    bias,
    stored_states,
    state_owner,
    burn_steps,
    valid_steps,
    cotangent,
):
    section_index = lax.axis_index("section")
    sections = lax.axis_size("section")
    step_count, seq_rows, breadth = obs_features.shape
    gate_width = 4 * breadth
    w_in = w_input[0]
    bias_row = bias[0]
    owned_rows = (state_owner == section_index)[None, :, None]
    state_table = jnp.where(owned_rows, stored_states[0].astype(jnp.float32), jnp.float32(0.0))
    delivered = lax.psum_scatter(
        state_table.astype(jnp.bfloat16), "section", scatter_dimension=0, tiled=True
    ).astype(jnp.float32)[0]
    hidden_start = delivered[:, :breadth].astype(jnp.bfloat16)
    cell_start = delivered[:, breadth:]
    w_rec = lax.all_gather(w_recurrent[0], "dp", axis=1, tiled=True)
    positions = jnp.arange(step_count, dtype=jnp.int32)[:, None]
    live_mask = ((positions >= burn_steps[None, :]) & (positions < valid_steps[None, :])).astype(
        jnp.float32
    )
    block_total = 1
    block_len = step_count // block_total
    tick_count = block_total + sections - 1

    def advance_block(inputs, offset, carried):
        hidden_now, cell_now, hidden_buf, cell_buf, gate_buf = carried
        hidden_seq, cell_seq, gate_seq, hidden_end, cell_end = forward_span(
            inputs, w_in, w_rec, bias_row, hidden_now, cell_now
        )
        hidden_buf = hidden_seq
        cell_buf = cell_seq
        gate_buf = gate_seq
        return ((hidden_end, cell_end, hidden_buf, cell_buf, gate_buf), hidden_seq)

    def keep_block(carried):
        return (carried, jnp.zeros((block_len, seq_rows, breadth), jnp.bfloat16))

    carried = (
        hidden_start,
        cell_start,
        jnp.zeros((step_count, seq_rows, breadth), jnp.bfloat16),
        jnp.zeros((step_count, seq_rows, breadth), jnp.float32),
        jnp.zeros((step_count, seq_rows, gate_width), jnp.float32),
    )
    incoming = jnp.zeros((block_len, seq_rows, breadth), jnp.bfloat16)
    for tick_index in range(tick_count):
        block_index = tick_index - section_index
        active = (block_index >= 0) & (block_index < block_total)
        offset = jnp.clip(block_index, 0, block_total - 1) * block_len
        inputs = jnp.where(section_index == 0, obs_features, incoming)
        carried, outgoing = lax.cond(
            active, partial(advance_block, inputs, offset), keep_block, carried
        )
        if tick_index + 1 < tick_count:
            incoming = from_behind(outgoing, "section", 1)
    hidden_buf = carried[2]
    cell_buf = carried[3]
    gate_buf = carried[4]
    cell_full = jnp.concatenate([cell_start[None], cell_buf], axis=0)

    def retreat_block(above_grads, offset, back_state):
        grad_h, grad_c, grad_buf = back_state
        cell_before = lax.dynamic_slice_in_dim(cell_full, offset, block_len, 0)
        gate_grads, grad_h, grad_c = backward_span(
            above_grads, cell_buf, cell_before, gate_buf, live_mask, w_rec, grad_h, grad_c
        )
        grad_buf = gate_grads

        def lower_input(values):
            return (
                times_transposed(values.reshape(-1, gate_width), w_in)
                .reshape(block_len, seq_rows, breadth)
                .astype(jnp.bfloat16)
            )

        def no_input(values):
            return jnp.zeros((block_len, seq_rows, breadth), jnp.bfloat16)

        lower_grads = lax.cond(section_index > 0, lower_input, no_input, gate_grads)
        return ((grad_h, grad_c, grad_buf), lower_grads)

    def keep_back(back_state):
        return (back_state, jnp.zeros((block_len, seq_rows, breadth), jnp.bfloat16))

    back_state = (
        jnp.zeros((seq_rows, breadth), jnp.float32),
        jnp.zeros((seq_rows, breadth), jnp.float32),
        jnp.zeros((step_count, seq_rows, gate_width), jnp.bfloat16),
    )
    arriving = jnp.zeros((block_len, seq_rows, breadth), jnp.bfloat16)
    for tick_index in range(tick_count):
        block_index = block_total - 1 - (tick_index - (sections - 1 - section_index))
        active = (block_index >= 0) & (block_index < block_total)
        offset = jnp.clip(block_index, 0, block_total - 1) * block_len
        above_grads = jnp.where(section_index == sections - 1, cotangent, arriving)
        back_state, sending = lax.cond(
            active, partial(retreat_block, above_grads, offset), keep_back, back_state
        )
        if tick_index + 1 < tick_count:
            arriving = from_behind(sending, "section", -1)
    gate_rows = back_state[2].reshape(step_count * seq_rows, gate_width)
    prev_rows = jnp.concatenate([hidden_start[None], hidden_buf[:-1]], axis=0).reshape(
        step_count * seq_rows, breadth
    )
    grad_cols = lax.all_to_all(gate_rows, "dp", split_axis=1, concat_axis=0, tiled=True)
    weight_grad = lax.dot_general(
        lax.all_gather(prev_rows, "dp", axis=0, tiled=True),
        grad_cols,
        (((0,), (0,)), ((), ())),
        preferred_element_type=jnp.float32,
    )
    bias_grad = jnp.sum(grad_cols, axis=0, dtype=jnp.float32)
    return (hidden_buf[None], weight_grad[None], bias_grad[None])


def solution(mesh):
    in_specs = (
        P(None, "dp", None),
        P("section", None, None),
        P("section", None, "dp"),
        P("section", None),
        P("section", None, "dp", None),
        P("dp"),
        P("dp"),
        P("dp"),
        P(None, "dp", None),
    )
    out_specs = (P("section", None, "dp", None), P("section", None, "dp"), P("section", "dp"))
    return jax.shard_map(
        on_device, mesh=mesh, in_specs=in_specs, out_specs=out_specs, check_vma=False
    )
```

profile of v0, /device:TPU:0, one launch (start us, length us, event | category | flops | bytes accessed | tf_op | source)
XLA Modules:
  0.0 535.3 jit_solution(6151085582079981420)
XLA Ops:
  8.8 2.0 fusion.141
  11.5 24.8 %reduce-scatter.2.cloned.1.call-done = bf16[1,32,2048]{2,1,0:T(8,128)(2,1)} async-done(((bf16[4,32,2048]{2,1,0:T(8,128)(2,1)}), bf16[1,32,2048]{2,1,0:T(8,128)(2,1)}) %reduce-scatter.2.cloned.1.call-update) | async-done | bytes 131088 | tf_op jit(solution)/shard_map/reduce_scatter | solution.py:110
  37.2 103.6 %all-gather.6.cloned.1.call-done = bf16[1,1024,4096]{2,1,0:T(8,128)(2,1)} async-done(((bf16[1,1024,512]{2,1,0:T(8,128)(2,1)}), bf16[1,1024,4096]{2,1,0:T(8,128)(2,1)}) %all-gather.6.cloned.1.call-update) | async-done | bytes 8388624 | tf_op jit(solution)/shard_map/all_gather | solution.py:115
  140.8 34.2 %conditional.11 = (bf16[32,1024]{1,0:T(8,128)(2,1)S(1)}, f32[32,1024]{1,0:T(8,128)S(1)}, bf16[4,32,1024]{2,1,0:T(8,128)(2,1)}, f32[4,32,1024]{2,1,0:T(8,128)}, f32[4,32,4096]{2,1,0:T(8,128)}) conditional(s32[]{:T(128)} %convert_element_type.215, (bf16[32,1024]{1,0:T(8,128)(2,1)S(1)}, f32[32,1024]{1,0:T(8,128)S(1)}) %tuple.195, ...), branch_computations={%region_1.2_spmd, %region_2.5_spmd} | conditional | flops 1343979520 | bytes 23545560 | solution.py:150
  140.8 4.6 fusion.12
  145.5 29.5 %while.150 = (s32[]{:T(128)}, bf16[32,1024]{1,0:T(8,128)(2,1)S(1)}, f32[32,1024]{1,0:T(8,128)S(1)}, bf16[4,32,1024]{2,1,0:T(8,128)(2,1)}, f32[4,32,1024]{2,1,0:T...) while((s32[]{:T(128)}, bf16[32,1024]{1,0:T(8,128)(2,1)S(1)}, ...), condition=%wide.region_4.4_spmd, body=%wide.region_3.3_spmd.sunk | while | flops 269713408 | bytes 12781153 | solution.py:39
  145.5 4.9 convolution_add_fusion.11
  152.9 4.9 convolution_add_fusion.11
  160.2 4.9 convolution_add_fusion.11
  167.6 4.9 convolution_add_fusion.11
  175.0 1.3 collective-permute-start
  176.3 1.3 collective-permute-done
  177.7 37.4 %collective-permute-start.1 = (bf16[4,32,1024]{2,1,0:T(8,128)(2,1)S(1)}, bf16[4,32,1024]{2,1,0:T(8,128)(2,1)S(1)}, u32[]{:S(2)}, u32[]{:S(2)}) collective-permute-start(bf16[4,32,1024]{2,1,0:T(8,128)(2,1)S(1)} %get-tuple-element.1425), channel_id=1, source_target_pairs={{0,8},{8,16},{16,24},{1,9},{9,17},{17,25},{2,10},{10,18},{18,26},{... | collective-permute-start | bytes 786440 | tf_op jit(solution)/shard_map/ppermute | solution.py:11
  216.3 4.1 collective-permute-start.2
  224.5 3.2 conditional.15
  227.7 1.3 collective-permute-start.3
  229.0 41.6 %collective-permute-done.3 = bf16[4,32,1024]{2,1,0:T(8,128)(2,1)S(1)} collective-permute-done((bf16[4,32,1024]{2,1,0:T(8,128)(2,1)}, bf16[4,32,1024]{2,1,0:T(8,128)(2,1)S(1)}, u32[]{:S(2)}, u32[]{:S(2)}) %collective-permute-start.3) | collective-permute-done | bytes 262176 | tf_op jit(solution)/shard_map/ppermute | solution.py:11
  272.6 7.3 %collective-permute-done.4 = bf16[4,32,1024]{2,1,0:T(8,128)(2,1)S(1)} collective-permute-done((bf16[4,32,1024]{2,1,0:T(8,128)(2,1)}, bf16[4,32,1024]{2,1,0:T(8,128)(2,1)S(1)}, u32[]{:S(2)}, u32[]{:S(2)}) %collective-permute-start.4) | collective-permute-done | bytes 262176 | tf_op jit(solution)/shard_map/ppermute | solution.py:11
  281.9 177.6 %collective-permute-done.5 = bf16[4,32,1024]{2,1,0:T(8,128)(2,1)S(1)} collective-permute-done((bf16[4,32,1024]{2,1,0:T(8,128)(2,1)}, bf16[4,32,1024]{2,1,0:T(8,128)(2,1)S(1)}, u32[]{:S(2)}, u32[]{:S(2)}) %collective-permute-start.5) | collective-permute-done | bytes 262176 | tf_op jit(solution)/shard_map/ppermute | solution.py:11
  459.5 42.7 %conditional.18 = (bf16[4,32,4096]{2,1,0:T(8,128)(2,1)}) conditional(s32[]{:T(128)} %convert_element_type.215, bf16[4,32,4096]{2,1,0:T(8,128)(2,1)} %get-tuple-element.1443, (pred[4,32,1024]{2,1,0:T(8,128)(4,1)S(1)}, bf16[4,32,1024]{2,1,0:T(8,128)(2,1)S(1)}, bf16[4,32,1024]{2,1,0:T(8,128)(2,1)S(1)}, s32[]{:T(128)}, f32[5,32,1024]{2,1,0:T(8,128)S(1)}, ...), branch_computations={%region_35.36_spmd, %region_36.39_spmd} | conditional | flops 270696448 | bytes 16057297 | solution.py:195
  460.8 41.5 %while.156 = (s32[]{:T(128)}, f32[32,1024]{1,0:T(8,128)}, f32[32,1024]{1,0:T(8,128)}, bf16[4,32,4096]{2,1,0:T(8,128)(2,1)}, bf16[4,32,1024]{2,1,0:T(8,128)(2,1)S...) while((s32[]{:T(128)}, f32[32,1024]{1,0:T(8,128)}, ...), condition=%wide.region_38.38_spmd, body=%wide.region_37.37_spmd.sunk | while | flops 270565376 | bytes 13042453 | solution.py:82
  461.9 1.8 multiply_multiply_fusion.8
  464.5 6.6 %fusion.206 = f32[32,1024]{1,0:T(8,128)} fusion(bf16[1024,4096]{1,0:T(8,128)(2,1)} %get-tuple-element.2300, f32[32,1024]{1,0:T(8,128)S(1)} %get-tuple-element.2149, f32[32,1024]{1,0:T(8,128)S(1)} %get-tuple-element.2151, f32[32,1024]{1,0:T(8,128)S(1)} %get-tuple-element.2152, f32[32,1024]{1,0:T(8,128)S(1)} %get-tuple-element.2153, f32[32]{0:T(128)S(1)} %fusion.205), kind=kOutput, calls=%fused_computation.162.clone.1 | convolution fusion | flops 269090816 | bytes 9044096 | tf_op jit(solution)/shard_map/cond/branch_1_fun/while/body/eval_jaxpr/dot_general | solution.py:46
  472.2 1.8 multiply_multiply_fusion.8
  474.8 6.6 %fusion.206 = f32[32,1024]{1,0:T(8,128)} fusion(bf16[1024,4096]{1,0:T(8,128)(2,1)} %get-tuple-element.2300, f32[32,1024]{1,0:T(8,128)S(1)} %get-tuple-element.2149, f32[32,1024]{1,0:T(8,128)S(1)} %get-tuple-element.2151, f32[32,1024]{1,0:T(8,128)S(1)} %get-tuple-element.2152, f32[32,1024]{1,0:T(8,128)S(1)} %get-tuple-element.2153, f32[32]{0:T(128)S(1)} %fusion.205), kind=kOutput, calls=%fused_computation.162.clone.1 | convolution fusion | flops 269090816 | bytes 9044096 | tf_op jit(solution)/shard_map/cond/branch_1_fun/while/body/eval_jaxpr/dot_general | solution.py:46
  482.6 1.8 multiply_multiply_fusion.8
  485.2 6.6 %fusion.206 = f32[32,1024]{1,0:T(8,128)} fusion(bf16[1024,4096]{1,0:T(8,128)(2,1)} %get-tuple-element.2300, f32[32,1024]{1,0:T(8,128)S(1)} %get-tuple-element.2149, f32[32,1024]{1,0:T(8,128)S(1)} %get-tuple-element.2151, f32[32,1024]{1,0:T(8,128)S(1)} %get-tuple-element.2152, f32[32,1024]{1,0:T(8,128)S(1)} %get-tuple-element.2153, f32[32]{0:T(128)S(1)} %fusion.205), kind=kOutput, calls=%fused_computation.162.clone.1 | convolution fusion | flops 269090816 | bytes 9044096 | tf_op jit(solution)/shard_map/cond/branch_1_fun/while/body/eval_jaxpr/dot_general | solution.py:46
  492.9 1.8 multiply_multiply_fusion.8
  495.6 6.6 %fusion.206 = f32[32,1024]{1,0:T(8,128)} fusion(bf16[1024,4096]{1,0:T(8,128)(2,1)} %get-tuple-element.2300, f32[32,1024]{1,0:T(8,128)S(1)} %get-tuple-element.2149, f32[32,1024]{1,0:T(8,128)S(1)} %get-tuple-element.2151, f32[32,1024]{1,0:T(8,128)S(1)} %get-tuple-element.2152, f32[32,1024]{1,0:T(8,128)S(1)} %get-tuple-element.2153, f32[32]{0:T(128)S(1)} %fusion.205), kind=kOutput, calls=%fused_computation.162.clone.1 | convolution fusion | flops 269090816 | bytes 9044096 | tf_op jit(solution)/shard_map/cond/branch_1_fun/while/body/eval_jaxpr/dot_general | solution.py:46
  502.2 1.6 copy.14
  504.2 18.7 %all_to_all.19 = bf16[128,8,512]{2,0,1:T(8,128)(2,1)S(1)} all-to-all(bf16[128,8,512]{2,0,1:T(8,128)(2,1)S(1)} %copy.13), channel_id=1, replica_groups=mesh['section'=4,'dp'=8] {'dp'}, dimensions={1} | all-to-all | bytes 2097152 | tf_op jit(solution)/shard_map/all_to_all | solution.py:204
  523.6 4.2 convolution_bitcast_fusion
  (84 shorter events, 37.1 us)
Async XLA Ops:
  8.0 3.4 copy-start
  8.0 132.8 %copy-start.2 = (f32[1,4096]{1,0:T(1,128)S(1)}, f32[1,4096]{1,0:T(1,128)}, u32[]{:S(2)}) copy-start(f32[1,4096]{1,0:T(1,128)} %param.50) | copy-start | bytes 49156
  8.0 28.3 %reduce-scatter.2.cloned.1.call-start = ((), (), s32[]{:S(2)}) async-start(), calls=%async_computation.2 | async-start | bytes 655360 | tf_op jit(solution)/shard_map/reduce_scatter | solution.py:110
  10.8 130.0 %all-gather.6.cloned.1.call-start = ((), (), s32[]{:S(2)}) async-start(), calls=%async_computation.4 | async-start | bytes 9437184 | tf_op jit(solution)/shard_map/all_gather | solution.py:115
  11.4 512.3 %all-gather.4.cloned.1.call-start = ((), (), s32[]{:S(2)}) async-start(), calls=%async_computation.3 | async-start | bytes 2359296 | tf_op jit(solution)/shard_map/all_gather | solution.py:206
  175.0 2.6 collective-permute-start
  177.7 38.5 %collective-permute-start.1 = (bf16[4,32,1024]{2,1,0:T(8,128)(2,1)S(1)}, bf16[4,32,1024]{2,1,0:T(8,128)(2,1)S(1)}, u32[]{:S(2)}, u32[]{:S(2)}) collective-permute-start(bf16[4,32,1024]{2,1,0:T(8,128)(2,1)S(1)} %get-tuple-element.1425), channel_id=1, source_target_pairs={{0,8},{8,16},{16,24},{1,9},{9,17},{17,25},{2,10},{10,18},{18,26},{... | collective-permute-start | bytes 786440 | tf_op jit(solution)/shard_map/ppermute | solution.py:11
  216.3 5.2 collective-permute-start.2
  221.5 1.8 copy-start.3
  221.5 1.8 copy-start.4
  222.5 2.0 copy-start.1
  227.7 42.9 %collective-permute-start.3 = (bf16[4,32,1024]{2,1,0:T(8,128)(2,1)}, bf16[4,32,1024]{2,1,0:T(8,128)(2,1)S(1)}, u32[]{:S(2)}, u32[]{:S(2)}) collective-permute-start(bf16[4,32,1024]{2,1,0:T(8,128)(2,1)} %get-tuple-element.1438), channel_id=1, source_target_pairs={{8,0},{16,8},{24,16},{9,1},{17,9},{25,17},{10,2},{18,10},{26,18},{... | collective-permute-start | bytes 786440 | tf_op jit(solution)/shard_map/ppermute | solution.py:11
  271.3 8.6 %collective-permute-start.4 = (bf16[4,32,1024]{2,1,0:T(8,128)(2,1)}, bf16[4,32,1024]{2,1,0:T(8,128)(2,1)S(1)}, u32[]{:S(2)}, u32[]{:S(2)}) collective-permute-start(bf16[4,32,1024]{2,1,0:T(8,128)(2,1)} %get-tuple-element.1442), channel_id=1, source_target_pairs={{8,0},{16,8},{24,16},{9,1},{17,9},{25,17},{10,2},{18,10},{26,18},{... | collective-permute-start | bytes 786440 | tf_op jit(solution)/shard_map/ppermute | solution.py:11
  280.7 178.8 %collective-permute-start.5 = (bf16[4,32,1024]{2,1,0:T(8,128)(2,1)}, bf16[4,32,1024]{2,1,0:T(8,128)(2,1)S(1)}, u32[]{:S(2)}, u32[]{:S(2)}) collective-permute-start(bf16[4,32,1024]{2,1,0:T(8,128)(2,1)} %get-tuple-element.1444), channel_id=1, source_target_pairs={{8,0},{16,8},{24,16},{9,1},{17,9},{25,17},{10,2},{18,10},{26,18},{... | collective-permute-start | bytes 786440 | tf_op jit(solution)/shard_map/ppermute | solution.py:11
Sparse Core Ops, SparseCore 0:
  11.9 24.3 reduce-scatter.1
Sparse Core Ops, SparseCore 1:
  13.3 127.4 all-gather.5
  223.3 117.3 all-gather.3
where the time goes:
time: 536 us; the launch traced here: 535 us
  waiting for transfers between devices  359 us (67%)
  matrix products  55.1 us (10%)
  starting transfers between devices  46.8 us (9%)
  other arithmetic  26.7 us (5%)
  blocking collectives  18.7 us (3%)
  between operations  15.7 us (3%)
  local copies, waits for them, and re-layouts  13.2 us (2%)
    ppermute x6, waiting for transfers between devices, from_behind(): return lax.ppermute(array, axis, pairs)  230 us
    all_gather x1, waiting for transfers between devices, on_device(): w_rec = lax.all_gather(w_recurrent[0], 'dp', axis=1, tiled=True)  104 us
    ppermute x6, starting transfers between devices, from_behind(): return lax.ppermute(array, axis, pairs)  46.6 us
    dot_general x4, matrix products, times_transposed(): lax.dot_general(operand, matrix, (((1,), (1,)), ((), ())), preferred_elem...  26.6 us
    reduce_scatter x1, waiting for transfers between devices, on_device(): lax.psum_scatter(state_table.astype(jnp.bfloat16), 'section', scatter_dim...  24.8 us
    dot_general x4, matrix products, advance(): jnp.dot(hidden_prev, w_rec, preferred_element_type=jnp.float32)  19.7 us
    all_to_all x1, blocking collectives, on_device(): lax.all_to_all(gate_rows, 'dp', split_axis=1, concat_axis=0, tiled=True)  18.7 us
  transfers between devices with their start and end apart: 9, of which 8 were waited for; matrix products, arithmetic and copies ran while one was open for 10% of the time, Pallas kernels for 0%

commit v1 on v0

--- a/solution.py
+++ b/solution.py
@@ -112,7 +112,7 @@
     ).astype(jnp.float32)[0]
     hidden_start = delivered[:, :breadth].astype(jnp.bfloat16)
     cell_start = delivered[:, breadth:]
-    w_rec = lax.all_gather(w_recurrent[0], "dp", axis=1, tiled=True)
+    w_rec = jnp.concatenate(lax.all_gather(w_recurrent[0], "dp"), axis=1)
     positions = jnp.arange(step_count, dtype=jnp.int32)[:, None]
     live_mask = ((positions >= burn_steps[None, :]) & (positions < valid_steps[None, :])).astype(
         jnp.float32

time: 536 us -> 642 us (1.20)
  waiting for transfers between devices: 359 us -> 417 us
  local copies, waits for them, and re-layouts: 13.2 us -> 48 us
  starting transfers between devices: 46.8 us -> 58.5 us
    ppermute x6, waiting for transfers between devices: 230 us -> 289 us  [from_behind(): return lax.ppermute(array, axis, pairs)]
    another operation x10 -> x12, local copies, waits for them, and re-layouts: 5.81 us -> 29.2 us
    ppermute x6, starting transfers between devices: 46.6 us -> 58.3 us  [from_behind(): return lax.ppermute(array, axis, pairs)]
    all_gather x0 -> x1, local copies, waits for them, and re-layouts: none -> 11.5 us  [on_device(): w_rec = jnp.concatenate(lax.all_gather(w_recurrent[0], 'dp'), axis=1)]
where the time goes in v1:
time: 642 us; the launch traced here: 640 us
  waiting for transfers between devices  417 us (65%)
  starting transfers between devices  58.5 us (9%)
  matrix products  55.1 us (9%)
  local copies, waits for them, and re-layouts  48 us (7%)
  other arithmetic  26.7 us (4%)
  blocking collectives  18.6 us (3%)
  between operations  15.7 us (2%)
    ppermute x6, waiting for transfers between devices, from_behind(): return lax.ppermute(array, axis, pairs)  289 us
    all_gather x1, waiting for transfers between devices, on_device(): w_rec = jnp.concatenate(lax.all_gather(w_recurrent[0], 'dp'), axis=1)  103 us
    ppermute x6, starting transfers between devices, from_behind(): return lax.ppermute(array, axis, pairs)  58.3 us
    another operation x12, local copies, waits for them, and re-layouts  29.2 us
    dot_general x4, matrix products, times_transposed(): lax.dot_general(operand, matrix, (((1,), (1,)), ((), ())), preferred_elem...  26.6 us
    reduce_scatter x1, waiting for transfers between devices, on_device(): lax.psum_scatter(state_table.astype(jnp.bfloat16), 'section', scatter_dim...  24.8 us
    dot_general x4, matrix products, advance(): jnp.dot(hidden_prev, w_rec, preferred_element_type=jnp.float32)  19.7 us
    all_to_all x1, blocking collectives, on_device(): lax.all_to_all(gate_rows, 'dp', split_axis=1, concat_axis=0, tiled=True)  18.6 us
  transfers between devices with their start and end apart: 9, of which 8 were waited for; matrix products, arithmetic and copies ran while one was open for 10% of the time, Pallas kernels for 0%

profile of v1, /device:TPU:0, one launch (start us, length us, event | category | flops | bytes accessed | tf_op | source)
XLA Modules:
  0.0 639.9 jit_solution(13734489165237088000)
XLA Ops:
  8.8 2.0 fusion.141
  11.5 24.8 %reduce-scatter.2.cloned.1.call-done = bf16[1,32,2048]{2,1,0:T(8,128)(2,1)} async-done(((bf16[4,32,2048]{2,1,0:T(8,128)(2,1)}), bf16[1,32,2048]{2,1,0:T(8,128)(2,1)}) %reduce-scatter.2.cloned.1.call-update) | async-done | bytes 131088 | tf_op jit(solution)/shard_map/reduce_scatter | solution.py:110
  37.2 103.1 %all-gather.3.cloned.1.call-done = bf16[8,1024,512]{2,1,0:T(8,128)(2,1)} async-done(((bf16[1,1024,512]{2,1,0:T(8,128)(2,1)}), bf16[8,1024,512]{2,1,0:T(8,128)(2,1)}) %all-gather.3.cloned.1.call-update) | async-done | bytes 8388624 | tf_op jit(solution)/shard_map/all_gather | solution.py:115
  140.3 11.5 %copy.17 = bf16[8,1024,512]{1,2,0:T(8,128)(2,1)} copy(bf16[8,1024,512]{2,1,0:T(8,128)(2,1)} %all-gather.3.cloned.1.call-done) | data formatting | bytes 16777216 | tf_op jit(solution)/shard_map/all_gather | solution.py:115
  151.8 45.9 %conditional.11 = (bf16[32,1024]{1,0:T(8,128)(2,1)S(1)}, f32[32,1024]{1,0:T(8,128)S(1)}, bf16[4,32,1024]{2,1,0:T(8,128)(2,1)}, f32[4,32,1024]{2,1,0:T(8,128)}, f32[4,32,4096]{2,1,0:T(8,128)}) conditional(s32[]{:T(128)} %convert_element_type.215, (bf16[32,1024]{1,0:T(8,128)(2,1)S(1)}, f32[32,1024]{1,0:T(8,128)S(1)}) %tuple.195, ...), branch_computations={%region_1.2_spmd, %region_2.5_spmd} | conditional | flops 1343979520 | bytes 40322776 | solution.py:150
  151.8 11.7 %copy.18 = bf16[1024,4096]{1,0:T(8,128)(2,1)} copy(bf16[1024,4096]{0,1:T(8,128)(2,1)} %get-tuple-element.1510) | data formatting | bytes 16777216 | tf_op jit(solution)/shard_map
  163.5 4.6 fusion.12
  168.2 29.5 %while.150 = (s32[]{:T(128)}, bf16[32,1024]{1,0:T(8,128)(2,1)S(1)}, f32[32,1024]{1,0:T(8,128)S(1)}, bf16[4,32,1024]{2,1,0:T(8,128)(2,1)}, f32[4,32,1024]{2,1,0:T...) while((s32[]{:T(128)}, bf16[32,1024]{1,0:T(8,128)(2,1)S(1)}, ...), condition=%wide.region_4.4_spmd, body=%wide.region_3.3_spmd.sunk | while | flops 269713408 | bytes 12781153 | solution.py:39
  168.2 4.9 convolution_add_fusion.11
  175.6 4.9 convolution_add_fusion.11
  182.9 4.9 convolution_add_fusion.11
  190.3 4.9 convolution_add_fusion.11
  200.4 49.1 %collective-permute-start.1 = (bf16[4,32,1024]{2,1,0:T(8,128)(2,1)S(1)}, bf16[4,32,1024]{2,1,0:T(8,128)(2,1)S(1)}, u32[]{:S(2)}, u32[]{:S(2)}) collective-permute-start(bf16[4,32,1024]{2,1,0:T(8,128)(2,1)S(1)} %get-tuple-element.1425), channel_id=1, source_target_pairs={{0,8},{8,16},{16,24},{1,9},{9,17},{17,25},{2,10},{10,18},{18,26},{... | collective-permute-start | bytes 786440 | tf_op jit(solution)/shard_map/ppermute | solution.py:11
  250.7 4.1 collective-permute-start.2
  258.9 3.2 conditional.15
  263.3 53.3 %collective-permute-done.3 = bf16[4,32,1024]{2,1,0:T(8,128)(2,1)S(1)} collective-permute-done((bf16[4,32,1024]{2,1,0:T(8,128)(2,1)}, bf16[4,32,1024]{2,1,0:T(8,128)(2,1)S(1)}, u32[]{:S(2)}, u32[]{:S(2)}) %collective-permute-start.3) | collective-permute-done | bytes 262176 | tf_op jit(solution)/shard_map/ppermute | solution.py:11
  318.7 7.3 %collective-permute-done.4 = bf16[4,32,1024]{2,1,0:T(8,128)(2,1)S(1)} collective-permute-done((bf16[4,32,1024]{2,1,0:T(8,128)(2,1)}, bf16[4,32,1024]{2,1,0:T(8,128)(2,1)S(1)}, u32[]{:S(2)}, u32[]{:S(2)}) %collective-permute-start.4) | collective-permute-done | bytes 262176 | tf_op jit(solution)/shard_map/ppermute | solution.py:11
  328.0 224.5 %collective-permute-done.5 = bf16[4,32,1024]{2,1,0:T(8,128)(2,1)S(1)} collective-permute-done((bf16[4,32,1024]{2,1,0:T(8,128)(2,1)}, bf16[4,32,1024]{2,1,0:T(8,128)(2,1)S(1)}, u32[]{:S(2)}, u32[]{:S(2)}) %collective-permute-start.5) | collective-permute-done | bytes 262176 | tf_op jit(solution)/shard_map/ppermute | solution.py:11
  552.5 54.5 %conditional.18 = (bf16[4,32,4096]{2,1,0:T(8,128)(2,1)}) conditional(s32[]{:T(128)} %convert_element_type.215, bf16[4,32,4096]{2,1,0:T(8,128)(2,1)} %get-tuple-element.1443, (pred[4,32,1024]{2,1,0:T(8,128)(4,1)S(1)}, bf16[4,32,1024]{2,1,0:T(8,128)(2,1)S(1)}, bf16[4,32,1024]{2,1,0:T(8,128)(2,1)S(1)}, s32[]{:T(128)}, f32[5,32,1024]{2,1,0:T(8,128)S(1)}, ...), branch_computations={%region_35.36_spmd, %region_36.39_spmd} | conditional | flops 270696448 | bytes 32834512 | solution.py:195
  552.5 11.7 %copy.25 = bf16[1024,4096]{1,0:T(8,128)(2,1)} copy(bf16[1024,4096]{0,1:T(8,128)(2,1)} %get-tuple-element.1582) | data formatting | bytes 16777216 | tf_op jit(solution)/shard_map
  565.4 41.5 %while.156 = (s32[]{:T(128)}, f32[32,1024]{1,0:T(8,128)}, f32[32,1024]{1,0:T(8,128)}, bf16[4,32,4096]{2,1,0:T(8,128)(2,1)}, bf16[4,32,1024]{2,1,0:T(8,128)(2,1)S...) while((s32[]{:T(128)}, f32[32,1024]{1,0:T(8,128)}, ...), condition=%wide.region_38.38_spmd, body=%wide.region_37.37_spmd.sunk | while | flops 270565376 | bytes 13042453 | solution.py:82
  566.5 1.8 multiply_multiply_fusion.8
  569.2 6.6 %fusion.206 = f32[32,1024]{1,0:T(8,128)} fusion(bf16[1024,4096]{1,0:T(8,128)(2,1)} %get-tuple-element.2378, f32[32,1024]{1,0:T(8,128)S(1)} %get-tuple-element.2227, f32[32,1024]{1,0:T(8,128)S(1)} %get-tuple-element.2229, f32[32,1024]{1,0:T(8,128)S(1)} %get-tuple-element.2230, f32[32,1024]{1,0:T(8,128)S(1)} %get-tuple-element.2231, f32[32]{0:T(128)S(1)} %fusion.205), kind=kOutput, calls=%fused_computation.162.clone.1 | convolution fusion | flops 269090816 | bytes 9044096 | tf_op jit(solution)/shard_map/cond/branch_1_fun/while/body/eval_jaxpr/dot_general | solution.py:46
  576.9 1.8 multiply_multiply_fusion.8
  579.5 6.6 %fusion.206 = f32[32,1024]{1,0:T(8,128)} fusion(bf16[1024,4096]{1,0:T(8,128)(2,1)} %get-tuple-element.2378, f32[32,1024]{1,0:T(8,128)S(1)} %get-tuple-element.2227, f32[32,1024]{1,0:T(8,128)S(1)} %get-tuple-element.2229, f32[32,1024]{1,0:T(8,128)S(1)} %get-tuple-element.2230, f32[32,1024]{1,0:T(8,128)S(1)} %get-tuple-element.2231, f32[32]{0:T(128)S(1)} %fusion.205), kind=kOutput, calls=%fused_computation.162.clone.1 | convolution fusion | flops 269090816 | bytes 9044096 | tf_op jit(solution)/shard_map/cond/branch_1_fun/while/body/eval_jaxpr/dot_general | solution.py:46
  587.3 1.8 multiply_multiply_fusion.8
  589.9 6.6 %fusion.206 = f32[32,1024]{1,0:T(8,128)} fusion(bf16[1024,4096]{1,0:T(8,128)(2,1)} %get-tuple-element.2378, f32[32,1024]{1,0:T(8,128)S(1)} %get-tuple-element.2227, f32[32,1024]{1,0:T(8,128)S(1)} %get-tuple-element.2229, f32[32,1024]{1,0:T(8,128)S(1)} %get-tuple-element.2230, f32[32,1024]{1,0:T(8,128)S(1)} %get-tuple-element.2231, f32[32]{0:T(128)S(1)} %fusion.205), kind=kOutput, calls=%fused_computation.162.clone.1 | convolution fusion | flops 269090816 | bytes 9044096 | tf_op jit(solution)/shard_map/cond/branch_1_fun/while/body/eval_jaxpr/dot_general | solution.py:46
  597.6 1.8 multiply_multiply_fusion.8
  600.3 6.6 %fusion.206 = f32[32,1024]{1,0:T(8,128)} fusion(bf16[1024,4096]{1,0:T(8,128)(2,1)} %get-tuple-element.2378, f32[32,1024]{1,0:T(8,128)S(1)} %get-tuple-element.2227, f32[32,1024]{1,0:T(8,128)S(1)} %get-tuple-element.2229, f32[32,1024]{1,0:T(8,128)S(1)} %get-tuple-element.2230, f32[32,1024]{1,0:T(8,128)S(1)} %get-tuple-element.2231, f32[32]{0:T(128)S(1)} %fusion.205), kind=kOutput, calls=%fused_computation.162.clone.1 | convolution fusion | flops 269090816 | bytes 9044096 | tf_op jit(solution)/shard_map/cond/branch_1_fun/while/body/eval_jaxpr/dot_general | solution.py:46
  606.9 1.6 copy.27
  608.9 18.6 %all_to_all.19 = bf16[128,8,512]{2,0,1:T(8,128)(2,1)S(1)} all-to-all(bf16[128,8,512]{2,0,1:T(8,128)(2,1)S(1)} %copy.26), channel_id=1, replica_groups=mesh['section'=4,'dp'=8] {'dp'}, dimensions={1} | all-to-all | bytes 2097152 | tf_op jit(solution)/shard_map/all_to_all | solution.py:204
  628.3 4.2 convolution_bitcast_fusion
  (87 shorter events, 40.9 us)
Async XLA Ops:
  8.0 3.4 copy-start
  8.0 28.3 %reduce-scatter.2.cloned.1.call-start = ((), (), s32[]{:S(2)}) async-start(), calls=%async_computation.2 | async-start | bytes 655360 | tf_op jit(solution)/shard_map/reduce_scatter | solution.py:110
  10.8 129.5 %all-gather.3.cloned.1.call-start = ((), (), s32[]{:S(2)}) async-start(), calls=%async_computation.3 | async-start | bytes 9437184 | tf_op jit(solution)/shard_map/all_gather | solution.py:115
  11.4 616.9 %all-gather.5.cloned.1.call-start = ((), (), s32[]{:S(2)}) async-start(), calls=%async_computation.4 | async-start | bytes 2359296 | tf_op jit(solution)/shard_map/all_gather | solution.py:206
  37.2 114.6 %copy-start.2 = (f32[1,4096]{1,0:T(1,128)S(1)}, f32[1,4096]{1,0:T(1,128)}, u32[]{:S(2)}) copy-start(f32[1,4096]{1,0:T(1,128)} %param.50) | copy-start | bytes 49156
  197.7 2.6 collective-permute-start
  200.4 50.3 %collective-permute-start.1 = (bf16[4,32,1024]{2,1,0:T(8,128)(2,1)S(1)}, bf16[4,32,1024]{2,1,0:T(8,128)(2,1)S(1)}, u32[]{:S(2)}, u32[]{:S(2)}) collective-permute-start(bf16[4,32,1024]{2,1,0:T(8,128)(2,1)S(1)} %get-tuple-element.1425), channel_id=1, source_target_pairs={{0,8},{8,16},{16,24},{1,9},{9,17},{17,25},{2,10},{10,18},{18,26},{... | collective-permute-start | bytes 786440 | tf_op jit(solution)/shard_map/ppermute | solution.py:11
  250.7 5.2 collective-permute-start.2
  255.9 1.8 copy-start.3
  255.9 1.8 copy-start.4
  256.9 2.0 copy-start.1
  262.0 54.6 %collective-permute-start.3 = (bf16[4,32,1024]{2,1,0:T(8,128)(2,1)}, bf16[4,32,1024]{2,1,0:T(8,128)(2,1)S(1)}, u32[]{:S(2)}, u32[]{:S(2)}) collective-permute-start(bf16[4,32,1024]{2,1,0:T(8,128)(2,1)} %get-tuple-element.1438), channel_id=1, source_target_pairs={{8,0},{16,8},{24,16},{9,1},{17,9},{25,17},{10,2},{18,10},{26,18},{... | collective-permute-start | bytes 786440 | tf_op jit(solution)/shard_map/ppermute | solution.py:11
  317.4 8.6 %collective-permute-start.4 = (bf16[4,32,1024]{2,1,0:T(8,128)(2,1)}, bf16[4,32,1024]{2,1,0:T(8,128)(2,1)S(1)}, u32[]{:S(2)}, u32[]{:S(2)}) collective-permute-start(bf16[4,32,1024]{2,1,0:T(8,128)(2,1)} %get-tuple-element.1442), channel_id=1, source_target_pairs={{8,0},{16,8},{24,16},{9,1},{17,9},{25,17},{10,2},{18,10},{26,18},{... | collective-permute-start | bytes 786440 | tf_op jit(solution)/shard_map/ppermute | solution.py:11
  326.7 225.7 %collective-permute-start.5 = (bf16[4,32,1024]{2,1,0:T(8,128)(2,1)}, bf16[4,32,1024]{2,1,0:T(8,128)(2,1)S(1)}, u32[]{:S(2)}, u32[]{:S(2)}) collective-permute-start(bf16[4,32,1024]{2,1,0:T(8,128)(2,1)} %get-tuple-element.1444), channel_id=1, source_target_pairs={{8,0},{16,8},{24,16},{9,1},{17,9},{25,17},{10,2},{18,10},{26,18},{... | collective-permute-start | bytes 786440 | tf_op jit(solution)/shard_map/ppermute | solution.py:11
Sparse Core Ops, SparseCore 0:
  11.9 24.3 reduce-scatter.1
Sparse Core Ops, SparseCore 1:
  13.4 126.9 all-gather.2
  257.8 140.8 all-gather.4
